TPU v7x, 32 devices: a whole 2x2x4 slice. The times are simulated.
32 devices in a mesh: gx: 4 (over z), gy: 4 (over y, x), gz: 2 (over core).
Axes of the slice: x: 2, y: 2, z: 4, core: 2. Of those that a mesh axis runs over, the one named last changes fastest.
Arguments:
- forces: float32 [3, 64, 64, 256], P(None, 'gx', 'gy', 'gz'), may hold values from -8 to 8
- mass_shift: float32 [64, 64, 256], P('gx', 'gy', 'gz'), may hold values from 0.5 to 2
- deflation: float32 [16, 3, 64, 64, 256], P(None, None, 'gx', 'gy', 'gz'), may hold values from -0.01953125 to 0.01953125
- coarse_factor: float32 [512, 512], P('gz'), may hold values from -0.041033009 to 0.6, as said below
- coarse_slot: int32 [32], replicated, may hold values from 0 to 31, each once
Outputs:
- solution: float32 [3, 64, 64, 256], P(None, 'gx', 'gy', 'gz')
- residual: float32 [3, 64, 64, 256], P(None, 'gx', 'gy', 'gz')
- direction: float32 [3, 64, 64, 256], P(None, 'gx', 'gy', 'gz')
Inputs may be any that keep to these rules, and one draw needn't show every extreme that they name: `coarse_factor`: lower triangular: zero above the diagonal; diagonal entries between 0.3 and 0.6. `coarse_slot`: each subdomain has its own coarse position.
All inputs are finite; a program needn't handle non-finite values.
Results may differ from a plain program's by a relative error of at most 0.0003.
Values sent between devices are 32-bit elements; how exact they have to be, the bound alone decides.
A program may use at most 192 MiB of HBM per device.

v0:
```python
import jax
import jax.numpy as jnp
from jax import lax
from jax.sharding import PartitionSpec as P

SWEEPS = 3
ITERS = 4


shear_modulus = 0.25
lame_first = 0.375
relaxation = 0.6
highest = lax.Precision.HIGHEST
offsets_unit = ((1, 0, 0), (0, 1, 0), (0, 0, 1))


def with_halo(cells, sides, width):
    for axis, dim in sides:
        count = lax.axis_size(axis)
        ends = count - 1
        head = lax.slice_in_dim(cells, 0, width, axis=dim)
        tail = lax.slice_in_dim(cells, cells.shape[dim] - width, cells.shape[dim], axis=dim)
        cells = jnp.concatenate(
            [
                lax.ppermute(tail, axis, [(i, (i + 1) % count) for i in range(ends)]),
                cells,
                lax.ppermute(head, axis, [((i + 1) % count, i) for i in range(ends)]),
            ],
            axis=dim,
        )
    return cells


def from_root(block, axis, holder):
    block = jnp.where(lax.axis_index(axis) == holder, block, jnp.zeros_like(block))
    return lax.psum(block, axis)


def passed_along(x, axis, by):
    count = lax.axis_size(axis)
    pairs = [(i, i + by) for i in range(count) if 0 <= i + by < count]
    return lax.ppermute(x, axis, pairs)


def stencil(padded, mass_shift):
    size_x = padded.shape[1] - 2
    size_y = padded.shape[2] - 2
    size_z = padded.shape[3] - 2
    stiffer = lame_first + shear_modulus

    def neighbor(component, shift_x, shift_y, shift_z):
        return padded[
            component,
            1 + shift_x : 1 + shift_x + size_x,
            1 + shift_y : 1 + shift_y + size_y,
            1 + shift_z : 1 + shift_z + size_z,
        ]

    def moved(component, first_unit, second_unit, sign_first, sign_second):
        return neighbor(
            component,
            sign_first * first_unit[0] + sign_second * second_unit[0],
            sign_first * first_unit[1] + sign_second * second_unit[1],
            sign_first * first_unit[2] + sign_second * second_unit[2],
        )

    outputs = []
    for component in range(3):
        middle = neighbor(component, 0, 0, 0)
        summed = mass_shift * middle
        for axis_number in range(3):
            unit_step = offsets_unit[axis_number]
            second_diff = (
                moved(component, unit_step, unit_step, 1, 0)
                + moved(component, unit_step, unit_step, -1, 0)
                - 2.0 * middle
            )
            weight = shear_modulus + stiffer if axis_number == component else shear_modulus
            summed = summed - weight * second_diff
        own_unit = offsets_unit[component]
        for partner in range(3):
            if partner != component:
                partner_unit = offsets_unit[partner]
                mixed_term = (
                    moved(partner, own_unit, partner_unit, 1, 1)
                    - moved(partner, own_unit, partner_unit, 1, -1)
                    - moved(partner, own_unit, partner_unit, -1, 1)
                    + moved(partner, own_unit, partner_unit, -1, -1)
                )
                summed = summed - 0.25 * stiffer * mixed_term
        outputs.append(summed)
    return jnp.stack(outputs)


def operate(field, mass_shift):
    padded = with_halo(field, (("gx", 1), ("gy", 2), ("gz", 3)), 1)
    return stencil(padded, mass_shift)


def coarse_chain(ordered, coarse_factor):
    slab_rows = coarse_factor.shape[0]
    blocks = lax.axis_size("gz")
    gz_index = lax.axis_index("gz")
    slab_start = gz_index * slab_rows
    zero_index = jnp.zeros((), jnp.int32)
    diag_block = lax.dynamic_slice(coarse_factor, (zero_index, slab_start), (slab_rows, slab_rows))
    own_rhs = lax.dynamic_slice(ordered, (slab_start,), (slab_rows,))
    solved = jnp.zeros_like(ordered)
    for block_index in range(blocks):
        known_part = jnp.dot(coarse_factor, solved, precision=highest)
        candidate = jax.scipy.linalg.solve_triangular(diag_block, own_rhs - known_part, lower=True)
        solved_piece = from_root(candidate, "gz", block_index)
        solved = lax.dynamic_update_slice(solved, solved_piece, (block_index * slab_rows,))
    own_forward = lax.dynamic_slice(solved, (slab_start,), (slab_rows,))
    running = jnp.zeros_like(ordered)
    own_block = jnp.zeros((slab_rows,), jnp.float32)
    for block_index in range(blocks - 1, -1, -1):
        active = gz_index == block_index
        back_rhs = own_forward - lax.dynamic_slice(running, (slab_start,), (slab_rows,))
        candidate = jax.scipy.linalg.solve_triangular(diag_block, back_rhs, lower=True, trans=1)
        own_block = jnp.where(active, candidate, own_block)
        if block_index > 0:
            outgoing = jnp.where(
                active, running + jnp.dot(candidate, coarse_factor, precision=highest), running
            )
            running = passed_along(outgoing, "gz", -1)
    return lax.all_gather(own_block, "gz", axis=0, tiled=True)


def body(forces, mass_shift, deflation, coarse_factor, coarse_slot):
    diagonal = mass_shift + (6.0 * shear_modulus + 2.0 * (lame_first + shear_modulus))
    vectors = deflation.shape[0]
    subdomains = coarse_slot.shape[0]
    flat_vectors = deflation.reshape(vectors, -1)
    positions = jnp.arange(subdomains, dtype=jnp.int32)
    slot_table = (positions[:, None] == coarse_slot[None, :]).astype(jnp.float32)
    subdomain = (lax.axis_index("gx") * lax.axis_size("gy") + lax.axis_index("gy")) * lax.axis_size(
        "gz"
    ) + lax.axis_index("gz")
    own_slot = lax.dynamic_index_in_dim(coarse_slot, subdomain, 0, keepdims=False)
    solution = jnp.zeros_like(forces)
    residual = forces
    direction = forces
    image_dir = forces
    precond_prior = jnp.float32(1.0)
    step_prior = jnp.float32(1.0)
    for iteration in range(ITERS):
        local_sums = jnp.dot(flat_vectors, residual.reshape(-1), precision=highest)
        gathered = lax.all_gather(local_sums[None, :], ("gx", "gy", "gz"), axis=0, tiled=True)
        ordered = jnp.dot(slot_table, gathered, precision=highest).reshape(-1)
        coarse_values = coarse_chain(ordered, coarse_factor)
        own_weights = lax.dynamic_slice(coarse_values, (own_slot * vectors,), (vectors,))
        correction = jnp.dot(own_weights, flat_vectors, precision=highest).reshape(residual.shape)
        smooth = relaxation * residual / diagonal
        for sweep_index in range(SWEEPS - 1):
            smooth = smooth + relaxation * (residual - operate(smooth, mass_shift)) / diagonal
        preconditioned = correction + smooth
        z_image = operate(preconditioned, mass_shift)
        precond_norm, z_energy = lax.psum(
            (jnp.sum(residual * preconditioned), jnp.sum(preconditioned * z_image)),
            ("gx", "gy", "gz"),
        )
        if iteration == 0:
            step_size = precond_norm / z_energy
            direction = preconditioned
            image_dir = z_image
        else:
            momentum = precond_norm / precond_prior
            step_size = precond_norm / (z_energy - momentum * precond_norm / step_prior)
            direction = preconditioned + momentum * direction
            image_dir = z_image + momentum * image_dir
        solution = solution + step_size * direction
        residual = residual - step_size * image_dir
        precond_prior = precond_norm
        step_prior = step_size
    return (solution, residual, direction)


def solution(mesh):
    return jax.shard_map(
        body,
        mesh=mesh,
        in_specs=(
            P(None, "gx", "gy", "gz"),
            P("gx", "gy", "gz"),
            P(None, None, "gx", "gy", "gz"),
            P("gz", None),
            P(),
        ),
        out_specs=(P(None, "gx", "gy", "gz"), P(None, "gx", "gy", "gz"), P(None, "gx", "gy", "gz")),
        check_vma=False,
    )
```

profile of v0, /device:TPU:0, one launch (start us, length us, event | category | flops | bytes accessed | tf_op | source)
XLA Modules:
  0.0 899.8 jit_solution(13080732898473620551)
XLA Ops:
  3.3 4.0 while.32
  7.3 19.7 %custom-call.23 = f32[2,128,128]{1,2,0:T(8,128)S(1)} custom-call(f32[2,128,128]{2,1,0:T(8,128)S(1)} %get-tuple-element.108), custom_call_target="InvertDiagBlocksLowerTriangular" | custom-call | tf_op jit(solution)/shard_map/jit(_solve_triangular)/triangular_solve | solution.py:120
  27.0 12.4 %fusion.16 = f32[16]{0:T(128)S(1)} fusion(f32[3,16,16,128,1]{3,4,2,1,0:T(1,128)S(1)} %bitcast.2294, f32[16,3,16,16,128]{4,3,2,1,0:T(8,128)} %param.11), kind=kOutput, calls=%fused_computation.43 | convolution fusion | flops 18874368 | bytes 6684736 | tf_op jit(solution)/shard_map/dot_general | solution.py:148
  39.7 42.0 %all-reduce.4 = f32[512]{0:T(512)S(1)} all-reduce(f32[512]{0:T(512)S(1)} %dynamic-update-slice.18), channel_id=2, replica_groups=mesh['gx'=4,'gy'=4,'gz'=2] {'gx','gy','gz'}, use_global_device_ids=true, to_apply=%add.4 | all-reduce | flops 512 | bytes 4096
  92.5 5.1 collective-permute-start.2
  98.8 6.4 copy.455
  111.2 4.8 collective-permute-start.4
  130.5 4.5 collective-permute-start.8
  138.2 5.6 collective-permute-start.10
  143.9 7.3 fusion.6
  154.9 4.2 collective-permute-start.12
  168.5 4.5 collective-permute-start.14
  175.9 5.7 collective-permute-start.16
  195.2 43.6 %all-reduce.11 = (f32[]{:T(128)}, f32[]{:T(128)}) all-reduce(f32[]{:T(128)} %get-tuple-element.131, f32[]{:T(128)} %get-tuple-element.130), channel_id=1, replica_groups=mesh['gx'=4,'gy'=4,'gz'=2] {'gx','gy','gz'}, use_global_device_ids=true, to_apply=%region_3.6 | all-reduce | flops 2 | bytes 16 | tf_op jit(solution)/shard_map/psum | solution.py:159
  241.2 12.1 %fusion.19 = f32[16]{0:T(128)S(1)} fusion(f32[3,16,16,128,1]{3,4,2,1,0:T(1,128)S(1)} %bitcast.2295, f32[16,3,16,16,128]{4,3,2,1,0:T(8,128)} %param.11), kind=kOutput, calls=%fused_computation.44 | convolution fusion | flops 18874368 | bytes 6684736 | tf_op jit(solution)/shard_map/dot_general | solution.py:148
  253.5 41.5 %all-reduce.5 = f32[512]{0:T(512)S(1)} all-reduce(f32[512]{0:T(512)S(1)} %dynamic-update-slice.19), channel_id=3, replica_groups=mesh['gx'=4,'gy'=4,'gz'=2] {'gx','gy','gz'}, use_global_device_ids=true, to_apply=%add.5 | all-reduce | flops 512 | bytes 4096
  306.4 4.5 collective-permute-start.21
  313.8 4.8 collective-permute-start.23
  337.4 5.0 collective-permute-start.27
  345.6 5.4 collective-permute-start.29
  351.1 6.6 fusion.4
  364.5 4.4 collective-permute-start.31
  380.1 4.5 collective-permute-start.33
  387.5 5.7 collective-permute-start.35
  409.8 43.8 %all-reduce.10 = (f32[]{:T(128)}, f32[]{:T(128)}) all-reduce(f32[]{:T(128)} %get-tuple-element.129, f32[]{:T(128)} %get-tuple-element.128), channel_id=1, replica_groups=mesh['gx'=4,'gy'=4,'gz'=2] {'gx','gy','gz'}, use_global_device_ids=true, to_apply=%region_9.12 | all-reduce | flops 2 | bytes 16 | tf_op jit(solution)/shard_map/psum | solution.py:159
  460.1 12.1 %fusion.22 = f32[16]{0:T(128)S(1)} fusion(f32[3,16,16,128,1]{3,4,2,1,0:T(1,128)S(1)} %bitcast.2297, f32[16,3,16,16,128]{4,3,2,1,0:T(8,128)} %param.11), kind=kOutput, calls=%fused_computation.45 | convolution fusion | flops 18874368 | bytes 6684736 | tf_op jit(solution)/shard_map/dot_general | solution.py:148
  472.4 42.2 %all-reduce.6 = f32[512]{0:T(512)S(1)} all-reduce(f32[512]{0:T(512)S(1)} %dynamic-update-slice.20), channel_id=4, replica_groups=mesh['gx'=4,'gy'=4,'gz'=2] {'gx','gy','gz'}, use_global_device_ids=true, to_apply=%add.6 | all-reduce | flops 512 | bytes 4096
  525.5 4.5 collective-permute-start.40
  532.9 4.8 collective-permute-start.42
  557.6 5.0 collective-permute-start.46
  565.8 5.4 collective-permute-start.48
  571.3 7.3 fusion.2
  583.7 4.2 collective-permute-start.50
  598.2 4.6 collective-permute-start.52
  605.6 5.7 collective-permute-start.54
  618.0 4.4 collective-permute-start.56
  631.3 43.8 %all-reduce.9 = (f32[]{:T(128)}, f32[]{:T(128)}) all-reduce(f32[]{:T(128)} %get-tuple-element.127, f32[]{:T(128)} %get-tuple-element.126), channel_id=1, replica_groups=mesh['gx'=4,'gy'=4,'gz'=2] {'gx','gy','gz'}, use_global_device_ids=true, to_apply=%region_15.18 | all-reduce | flops 2 | bytes 16 | tf_op jit(solution)/shard_map/psum | solution.py:159
  680.1 12.1 %fusion.25 = f32[16]{0:T(128)S(1)} fusion(f32[3,16,16,128,1]{3,4,2,1,0:T(1,128)S(1)} %bitcast.2296, f32[16,3,16,16,128]{4,3,2,1,0:T(8,128)} %param.11), kind=kOutput, calls=%fused_computation.46 | convolution fusion | flops 18874368 | bytes 6684736 | tf_op jit(solution)/shard_map/dot_general | solution.py:148
  692.4 41.8 %all-reduce.7 = f32[512]{0:T(512)S(1)} all-reduce(f32[512]{0:T(512)S(1)} %dynamic-update-slice.21), channel_id=5, replica_groups=mesh['gx'=4,'gy'=4,'gz'=2] {'gx','gy','gz'}, use_global_device_ids=true, to_apply=%add.7 | all-reduce | flops 512 | bytes 4096
  745.0 4.5 collective-permute-start.59
  752.4 4.8 collective-permute-start.61
  777.1 5.0 collective-permute-start.65
  785.3 5.4 collective-permute-start.67
  790.7 6.6 fusion
  804.3 4.5 collective-permute-start.69
  818.8 4.6 collective-permute-start.71
  826.2 5.7 collective-permute-start.73
  849.6 43.8 %all-reduce.8 = (f32[]{:T(128)}, f32[]{:T(128)}) all-reduce(f32[]{:T(128)} %get-tuple-element.125, f32[]{:T(128)} %get-tuple-element.124), channel_id=1, replica_groups=mesh['gx'=4,'gy'=4,'gz'=2] {'gx','gy','gz'}, use_global_device_ids=true, to_apply=%region_21.24 | all-reduce | flops 2 | bytes 16 | tf_op jit(solution)/shard_map/psum | solution.py:159
  (598 shorter events, 295.2 us)
Async XLA Ops:
  89.8 19.3 %collective-permute-start = (f32[512]{0:T(512)S(1)}, f32[512]{0:T(512)S(1)}, u32[]{:S(2)}, u32[]{:S(2)}) collective-permute-start(f32[512]{0:T(512)S(1)} %broadcast_select_fusion.3), channel_id=1, source_target_pairs={{1,0},{3,2},{5,4},{7,6},{9,8},{11,10},{13,12},{15,14},{17,16},{19,... | collective-permute-start | bytes 6152 | tf_op jit(solution)/shard_map/ppermute | solution.py:42
  91.2 18.6 %collective-permute-start.1 = (f32[3,1,16,128]{3,2,1,0:T(8,128)S(1)}, f32[3,1,16,128]{3,2,1,0:T(8,128)S(1)}, u32[]{:S(2)}, u32[]{:S(2)}) collective-permute-start(f32[3,1,16,128]{3,2,1,0:T(8,128)S(1)} %get-tuple-element.278), channel_id=1, source_target_pairs={{8,0},{16,8},{24,16},{9,1},{17,9},{25,17},{10,2},{18,10},{26,18},{... | collective-permute-start | bytes 73736 | tf_op jit(solution)/shard_map/ppermute | solution.py:27
  92.5 17.3 %collective-permute-start.2 = (f32[3,1,16,128]{3,2,1,0:T(8,128)S(1)}, f32[3,1,16,128]{3,2,1,0:T(8,128)S(1)}, u32[]{:S(2)}, u32[]{:S(2)}) collective-permute-start(f32[3,1,16,128]{3,2,1,0:T(8,128)S(1)} %get-tuple-element.277), channel_id=1, source_target_pairs={{0,8},{8,16},{16,24},{1,9},{9,17},{17,25},{2,10},{10,18},{18,26},{... | collective-permute-start | bytes 73736 | tf_op jit(solution)/shard_map/ppermute | solution.py:25
  111.2 6.3 collective-permute-start.4
  129.2 7.7 collective-permute-start.7
  130.5 6.4 collective-permute-start.8
  136.9 14.3 %collective-permute-start.9 = (f32[3,18,1,128]{3,2,1,0:T(1,128)S(1)}, f32[3,18,1,128]{3,2,1,0:T(1,128)S(1)}, u32[]{:S(2)}, u32[]{:S(2)}) collective-permute-start(f32[3,18,1,128]{3,2,1,0:T(1,128)S(1)} %get-tuple-element.250), channel_id=1, source_target_pairs={{2,0},{4,2},{6,4},{3,1},{5,3},{7,5},{10,8},{12,10},{14,12},{11,9},... | collective-permute-start | bytes 82952 | tf_op jit(solution)/shard_map/ppermute | solution.py:27
  138.2 13.0 %collective-permute-start.10 = (f32[3,18,1,128]{3,2,1,0:T(1,128)S(1)}, f32[3,18,1,128]{3,2,1,0:T(1,128)S(1)}, u32[]{:S(2)}, u32[]{:S(2)}) collective-permute-start(f32[3,18,1,128]{3,2,1,0:T(1,128)S(1)} %get-tuple-element.249), channel_id=1, source_target_pairs={{0,2},{2,4},{4,6},{1,3},{3,5},{5,7},{8,10},{10,12},{12,14},{9,11},... | collective-permute-start | bytes 82952 | tf_op jit(solution)/shard_map/ppermute | solution.py:25
  152.6 6.6 collective-permute-start.11
  154.9 6.4 collective-permute-start.12
  174.6 7.1 collective-permute-start.15
  175.9 7.3 collective-permute-start.16
  303.2 7.7 collective-permute-start.19
  305.1 6.5 collective-permute-start.20
  312.5 6.7 collective-permute-start.22
  336.1 8.1 collective-permute-start.26
  337.4 6.8 collective-permute-start.27
  344.3 13.4 %collective-permute-start.28 = (f32[3,18,1,128]{3,2,1,0:T(1,128)S(1)}, f32[3,18,1,128]{3,2,1,0:T(1,128)S(1)}, u32[]{:S(2)}, u32[]{:S(2)}) collective-permute-start(f32[3,18,1,128]{3,2,1,0:T(1,128)S(1)} %get-tuple-element.238), channel_id=1, source_target_pairs={{2,0},{4,2},{6,4},{3,1},{5,3},{7,5},{10,8},{12,10},{14,12},{11,9},... | collective-permute-start | bytes 82952 | tf_op jit(solution)/shard_map/ppermute | solution.py:27
  345.6 12.1 %collective-permute-start.29 = (f32[3,18,1,128]{3,2,1,0:T(1,128)S(1)}, f32[3,18,1,128]{3,2,1,0:T(1,128)S(1)}, u32[]{:S(2)}, u32[]{:S(2)}) collective-permute-start(f32[3,18,1,128]{3,2,1,0:T(1,128)S(1)} %get-tuple-element.237), channel_id=1, source_target_pairs={{0,2},{2,4},{4,6},{1,3},{3,5},{5,7},{8,10},{10,12},{12,14},{9,11},... | collective-permute-start | bytes 82952 | tf_op jit(solution)/shard_map/ppermute | solution.py:25
  362.2 8.6 collective-permute-start.30
  364.5 8.3 collective-permute-start.31
  386.2 7.1 collective-permute-start.34
  387.5 7.3 collective-permute-start.35
  522.8 7.2 collective-permute-start.38
  524.2 6.5 collective-permute-start.39
  542.1 7.1 collective-permute-start.43
  556.4 8.1 collective-permute-start.45
  557.6 6.8 collective-permute-start.46
  564.5 14.1 %collective-permute-start.47 = (f32[3,18,1,128]{3,2,1,0:T(1,128)S(1)}, f32[3,18,1,128]{3,2,1,0:T(1,128)S(1)}, u32[]{:S(2)}, u32[]{:S(2)}) collective-permute-start(f32[3,18,1,128]{3,2,1,0:T(1,128)S(1)} %get-tuple-element.226), channel_id=1, source_target_pairs={{2,0},{4,2},{6,4},{3,1},{5,3},{7,5},{10,8},{12,10},{14,12},{11,9},... | collective-permute-start | bytes 82952 | tf_op jit(solution)/shard_map/ppermute | solution.py:27
  565.8 12.8 %collective-permute-start.48 = (f32[3,18,1,128]{3,2,1,0:T(1,128)S(1)}, f32[3,18,1,128]{3,2,1,0:T(1,128)S(1)}, u32[]{:S(2)}, u32[]{:S(2)}) collective-permute-start(f32[3,18,1,128]{3,2,1,0:T(1,128)S(1)} %get-tuple-element.225), channel_id=1, source_target_pairs={{0,2},{2,4},{4,6},{1,3},{3,5},{5,7},{8,10},{10,12},{12,14},{9,11},... | collective-permute-start | bytes 82952 | tf_op jit(solution)/shard_map/ppermute | solution.py:25
  581.4 7.6 collective-permute-start.49
  583.7 7.3 collective-permute-start.50
  604.3 7.1 collective-permute-start.53
  605.6 7.3 collective-permute-start.54
  615.7 7.7 collective-permute-start.55
  618.0 7.4 collective-permute-start.56
  742.4 7.2 collective-permute-start.57
  743.7 6.5 collective-permute-start.58
  761.7 7.1 collective-permute-start.62
  775.8 8.1 collective-permute-start.64
  777.1 6.8 collective-permute-start.65
  784.0 13.4 %collective-permute-start.66 = (f32[3,18,1,128]{3,2,1,0:T(1,128)S(1)}, f32[3,18,1,128]{3,2,1,0:T(1,128)S(1)}, u32[]{:S(2)}, u32[]{:S(2)}) collective-permute-start(f32[3,18,1,128]{3,2,1,0:T(1,128)S(1)} %get-tuple-element.214), channel_id=1, source_target_pairs={{2,0},{4,2},{6,4},{3,1},{5,3},{7,5},{10,8},{12,10},{14,12},{11,9},... | collective-permute-start | bytes 82952 | tf_op jit(solution)/shard_map/ppermute | solution.py:27
  785.3 12.1 %collective-permute-start.67 = (f32[3,18,1,128]{3,2,1,0:T(1,128)S(1)}, f32[3,18,1,128]{3,2,1,0:T(1,128)S(1)}, u32[]{:S(2)}, u32[]{:S(2)}) collective-permute-start(f32[3,18,1,128]{3,2,1,0:T(1,128)S(1)} %get-tuple-element.213), channel_id=1, source_target_pairs={{0,2},{2,4},{4,6},{1,3},{3,5},{5,7},{8,10},{10,12},{12,14},{9,11},... | collective-permute-start | bytes 82952 | tf_op jit(solution)/shard_map/ppermute | solution.py:25
  800.9 8.8 collective-permute-start.68
  804.3 7.5 collective-permute-start.69
  824.9 7.1 collective-permute-start.72
  826.2 7.3 collective-permute-start.73
  836.4 6.8 collective-permute-start.74
  (98 other events, 988.5 us)
where the time goes:
time: 912 us; the launch traced here: 900 us
  blocking collectives  369 us (40%)
  starting transfers between devices  216 us (24%)
  local copies, waits for them, and re-layouts  102 us (11%)
  matrix products  91.4 us (10%)
  other arithmetic  83.8 us (9%)
  waiting for transfers between devices  20.2 us (2%)
  between operations  17.1 us (2%)
    psum x4, blocking collectives, body(): lax.psum((jnp.sum(residual * preconditioned), jnp.sum(preconditioned * z_...  175 us
    unnamed x4, blocking collectives  167 us
    ppermute x36, starting transfers between devices, with_halo(): lax.ppermute(tail, axis, [(i, (i + 1) % count) for i in range(ends)])  164 us
    dot_general x4, matrix products, body(): local_sums = jnp.dot(flat_vectors, residual.reshape(-1), precision=highest)  48.7 us
    unnamed x174, local copies, waits for them, and re-layouts  46.4 us
    ppermute x36, starting transfers between devices, with_halo(): lax.ppermute(head, axis, [((i + 1) % count, i) for i in range(ends)])  46.3 us
    concatenate x48, other arithmetic, with_halo(): jnp.concatenate([lax.ppermute(tail, axis, [(i, (i + 1) % count) for i in...  37.7 us
    dot_general x4, matrix products, body(): jnp.dot(own_weights, flat_vectors, precision=highest)  27.9 us
  transfers between devices with their start and end apart: 76, of which 16 were waited for; matrix products, arithmetic and copies ran while one was open for 9% of the time, Pallas kernels for 0%

commit v1 on v0

v1 whole, which is shorter than its diff:
```python
import functools

import jax
import jax.numpy as jnp
from jax import lax
from jax.experimental import pallas as pl
from jax.experimental.pallas import tpu as pltpu
from jax.sharding import PartitionSpec as P

SWEEPS = 3
ITERS = 4
MESH = pl.DeviceIdType.MESH
HIGHEST = lax.Precision.HIGHEST
W = 3
LEAD = 4
DIRS = tuple((dx, dy) for dx in (-1, 0, 1) for dy in (-1, 0, 1) if (dx, dy) != (0, 0))
BLOCK = 128


def dot(a, b):
    return jnp.dot(a, b, precision=HIGHEST, preferred_element_type=jnp.float32)


def kernel(
    sizes,
    forces, mass, defl, factor, slot_column,
    sol, res, direc,
    zext, rext, idir, cext, mext, cor, ua, ub, uz, vx,
    low, high, got_low, got_high,
    low_c, high_c, got_low_c, got_high_c,
    low_m, high_m, got_low_m, got_high_m,
    zsend, zgot, vzb,
    full, inv, sol_mat, gsend, gat, gres, gdir,
    zx_send, zx_recv, c_send, c_recv, m_send, m_recv,
    zc_send, zc_recv, g_send, g_recv, f_send, f_recv, f_local,
):
    nx, ny, nz, cx, cy, vectors, order = sizes
    n = nx * ny * nz
    ex = cx + 2 * LEAD
    ey = cy + 8
    gx, gy, gz = lax.axis_index("gx"), lax.axis_index("gy"), lax.axis_index("gz")
    me = (gx * ny + gy) * nz + gz
    f32 = jnp.float32

    def coords(t):
        return {"gx": t // (ny * nz), "gy": (t // nz) % ny, "gz": t % nz}

    lane = lax.broadcasted_iota(jnp.int32, (ey, 128), 1)
    row8 = lax.broadcasted_iota(jnp.int32, (8, 128), 0)
    rows = lax.broadcasted_iota(jnp.int32, (ey, 128), 0)
    lane1 = lax.broadcasted_iota(jnp.int32, (1, 128), 1)

    for ref in (zext, cor, mext, got_low, got_high, got_low_c, got_high_c, got_low_m, got_high_m):
        lead = ref.shape[0]
        for c in range(lead):
            def clear(i, _, ref=ref, c=c):
                ref[c, i] = jnp.zeros(ref.shape[2:], f32)
                return 0
            lax.fori_loop(0, ref.shape[1], clear, 0)
    zgot[...] = jnp.zeros(zgot.shape, f32)

    barrier = pltpu.get_barrier_semaphore()

    def greet(j, _):
        t = lax.rem(me + j, n)
        pl.semaphore_signal(barrier, inc=1, device_id=coords(t), device_id_type=MESH)
        return 0

    lax.fori_loop(1, n, greet, 0)
    pl.semaphore_wait(barrier, n - 1)

    slab = order // nz

    def slab_copy(j):
        t = lax.rem(gz + j, nz)
        return pltpu.make_async_remote_copy(
            src_ref=factor,
            dst_ref=full.at[gz],
            send_sem=f_send.at[j - 1],
            recv_sem=f_recv.at[j - 1],
            device_id={"gx": gx, "gy": gy, "gz": t},
            device_id_type=MESH,
        )

    for j in range(1, nz):
        slab_copy(j).start()
    own_slab = pltpu.make_async_copy(factor, full.at[gz], f_local)
    own_slab.start()

    def exists(dx, dy):
        ok = jnp.bool_(True)
        if dx < 0:
            ok = jnp.logical_and(ok, gx > 0)
        if dx > 0:
            ok = jnp.logical_and(ok, gx < nx - 1)
        if dy < 0:
            ok = jnp.logical_and(ok, gy > 0)
        if dy > 0:
            ok = jnp.logical_and(ok, gy < ny - 1)
        return ok

    def pieces(ext, lo, hi, glo, ghi, send, recv):
        half = cx // 2
        out = []
        for d, (dx, dy) in enumerate(DIRS):
            if dy == 0:
                src = ext.at[:, pl.ds(LEAD if dx < 0 else LEAD + cx - W, W), pl.ds(0, cy)]
                dst = ext.at[:, pl.ds(LEAD + cx if dx < 0 else LEAD - W, W), pl.ds(0, cy)]
            else:
                start, count = {0: (0, half), -1: (0, 2), 1: (half - 2, 2)}[dx]
                to = {0: 2, -1: 2 + half, 1: 0}[dx]
                src = (lo if dy < 0 else hi).at[:, pl.ds(start, count)]
                dst = (glo if dy < 0 else ghi).at[:, pl.ds(to, count)]
            copy = pltpu.make_async_remote_copy(
                src_ref=src,
                dst_ref=dst,
                send_sem=send.at[d],
                recv_sem=recv.at[d],
                device_id={"gx": gx + dx, "gy": gy + dy, "gz": gz},
                device_id_type=MESH,
            )
            out.append((dx, dy, copy))
        return out

    def send_halo(ext, lo, hi, glo, ghi, send, recv):
        def pack(i, _):
            for c in range(ext.shape[0]):
                even, odd = LEAD + 2 * i, LEAD + 2 * i + 1
                lo[c, i] = jnp.where(row8 < 4, ext[c, even, 0:8], pltpu.roll(ext[c, odd, 0:8], 4, 0))
                hi[c, i] = jnp.where(
                    row8 >= 4, ext[c, even, cy - 8 : cy], pltpu.roll(ext[c, odd, cy - 8 : cy], 4, 0)
                )
            return 0

        lax.fori_loop(0, cx // 2, pack, 0)
        for dx, dy, copy in pieces(ext, lo, hi, glo, ghi, send, recv):
            pl.when(exists(dx, dy))(copy.start)

    def take_halo(ext, lo, hi, glo, ghi, send, recv):
        for dx, dy, copy in pieces(ext, lo, hi, glo, ghi, send, recv):
            pl.when(exists(-dx, -dy))(copy.wait_recv)
            pl.when(exists(dx, dy))(copy.wait_send)

        def unpack(i, _):
            for c in range(ext.shape[0]):
                a, b = glo[c, i], ghi[c, i]
                ext[c, 2 * i, cy : cy + 8] = jnp.where(row8 < 4, a, b)
                ext[c, 2 * i + 1, cy : cy + 8] = jnp.where(
                    row8 < 4, pltpu.roll(a, 4, 0), pltpu.roll(b, 4, 0)
                )
            return 0

        lax.fori_loop(0, ex // 2, unpack, 0)

    halo_z = (zext, low, high, got_low, got_high, zx_send, zx_recv)
    halo_c = (cor, low_c, high_c, got_low_c, got_high_c, c_send, c_recv)
    halo_m = (mext, low_m, high_m, got_low_m, got_high_m, m_send, m_recv)

    def columns(stage, side):
        return pltpu.make_async_remote_copy(
            src_ref=zsend.at[stage, side],
            dst_ref=zgot.at[stage, 1 - side],
            send_sem=zc_send.at[stage, side],
            recv_sem=zc_recv.at[stage, side],
            device_id={"gx": gx, "gy": gy, "gz": gz + (2 * side - 1)},
            device_id_type=MESH,
        )

    has = (gz > 0, gz < nz - 1)

    def exchange_columns(u, stage, first, last):
        for side in (0, 1):
            @pl.when(has[side])
            def _(side=side):
                def gather(x, acc):
                    shift = x if side == 0 else x + 1
                    return tuple(
                        jnp.where(lane == x, pltpu.roll(u[c, x], shift, 1), acc[c]) for c in range(3)
                    )

                acc = lax.fori_loop(first, last, gather, (jnp.zeros((ey, 128), f32),) * 3, unroll=2)
                for c in range(3):
                    zsend[stage, side, c] = acc[c]
                columns(stage, side).start()
        for side in (0, 1):
            pl.when(has[1 - side])(columns(stage, side).wait_recv)
            pl.when(has[side])(columns(stage, side).wait_send)
        for side in (0, 1):
            bx, by = zgot[stage, side, 0], zgot[stage, side, 1]
            vzb[side] = (
                pltpu.roll(bx, 127, 1) - pltpu.roll(bx, 1, 1)
                + pltpu.roll(by, ey - 1, 0) - pltpu.roll(by, 1, 0)
            )

    def y_pair(v):
        return pltpu.roll(v, ey - 1, 0), pltpu.roll(v, 1, 0)

    def z_pair(v, upper, lower, x):
        up = jnp.where(lane == 127, pltpu.roll(upper, 127 - x, 1), pltpu.roll(v, 127, 1))
        down = jnp.where(lane == 0, pltpu.roll(lower, 128 - x, 1), pltpu.roll(v, 1, 1))
        return up, down

    def off_diagonal(u, stage, first, last, use, carry):
        def before(x, _):
            p, m = y_pair(u[1, x])
            q, r = z_pair(u[2, x], zgot[stage, 1, 2], zgot[stage, 0, 2], x)
            vx[x] = (p - m) + (q - r)
            return 0

        lax.fori_loop(first - 1, last + 1, before, 0, unroll=2)

        def at(x, carry):
            pair, diff = [], []
            for c in range(3):
                v = u[c, x]
                xp, xm = u[c, x + 1], u[c, x - 1]
                yp, ym = y_pair(v)
                zp, zm = z_pair(v, zgot[stage, 1, c], zgot[stage, 0, c], x)
                pair.append((xp + xm, yp + ym, zp + zm))
                diff.append(((xp - xm), (yp - ym), (zp - zm))[c])
            px, py, pz = diff
            dx = vx[x + 1] - vx[x - 1]
            yp, ym = y_pair(px + pz)
            zp, zm = z_pair(px + py, vzb[1], vzb[0], x)
            mixed = (dx, yp - ym, zp - zm)
            off = tuple(
                0.25 * (pair[c][0] + pair[c][1] + pair[c][2]) + 0.625 * pair[c][c] + 0.15625 * mixed[c]
                for c in range(3)
            )
            return use(x, off, carry)

        return lax.fori_loop(first, last, at, carry)

    base = lax.rem(me, 8) * vectors if vectors * 8 == 128 else 0

    def share(slot, gamma, energy):
        def part(x, acc):
            acc = list(acc)
            for c in range(3):
                v = zext[c, LEAD + x, 0:cy]
                for k in range(vectors):
                    prod = defl[k, c, x] * v
                    for t in range(0, cy, 8):
                        acc[k] = acc[k] + prod[t : t + 8]
            return tuple(acc)

        acc = lax.fori_loop(0, cx, part, (jnp.zeros((8, 128), f32),) * vectors)
        line = jnp.zeros((1, 128), f32)
        for k in range(vectors):
            total = jnp.sum(jnp.sum(acc[k], axis=0, keepdims=True), axis=1, keepdims=True)
            line = jnp.where(lane1 == base + k, total, line)
        gsend[slot, 0:1] = line
        gsend[slot, 1:2] = jnp.where(lane1 == 0, gamma, jnp.where(lane1 == 1, energy, 0.0))
        gat[slot, me] = gsend[slot]

        def push(j, _):
            t = lax.rem(me + j, n)
            pltpu.make_async_remote_copy(
                src_ref=gsend.at[slot],
                dst_ref=gat.at[slot, me],
                send_sem=g_send.at[slot],
                recv_sem=g_recv.at[slot, me],
                device_id=coords(t),
                device_id_type=MESH,
            ).start()
            return 0

        lax.fori_loop(1, n, push, 0)

    def collect(slot):
        def await_one(j, _):
            t = lax.rem(me + j, n)
            pltpu.make_async_copy(gsend.at[slot], gat.at[slot, t], g_recv.at[slot, t]).wait()
            return 0

        lax.fori_loop(1, n, await_one, 0)
        pltpu.make_async_copy(
            gat.at[slot, pl.ds(0, n - 1)], gat.at[slot, pl.ds(0, n - 1)], g_send.at[slot]
        ).wait()
        lines, scal = [], jnp.zeros((1, 128), f32)
        for t in range(n // 8):
            both = jnp.zeros((2, 128), f32)
            for s in range(8):
                both = both + gat[slot, 8 * t + s]
            lines.append(both[0:1])
            scal = scal + both[1:2]
        gamma = jnp.sum(jnp.where(lane1 == 0, scal, 0.0), axis=1, keepdims=True)
        energy = jnp.sum(jnp.where(lane1 == 1, scal, 0.0), axis=1, keepdims=True)
        return lines, gamma, energy

    def fill(x, _):
        for c in range(3):
            zext[c, LEAD + x, 0:cy] = forces[c, x]
            sol[c, x] = jnp.zeros((cy, 128), f32)
            direc[c, x] = jnp.zeros((cy, 128), f32)
        mext[0, LEAD + x, 0:cy] = mass[x]
        return 0

    lax.fori_loop(0, cx, fill, 0)
    send_halo(*halo_z)
    send_halo(*halo_m)
    zero = jnp.zeros((1, 1), f32)
    share(0, zero, zero)

    for j in range(1, nz):
        copy = slab_copy(j)
        copy.wait_recv()
        copy.wait_send()
    own_slab.wait()
    per_slab = slab // BLOCK
    blocks = order // BLOCK
    group = min(4, blocks)
    r_i = lax.broadcasted_iota(jnp.int32, (BLOCK, BLOCK), 0)
    c_i = lax.broadcasted_iota(jnp.int32, (BLOCK, BLOCK), 1)

    def invert(g, _):
        lows, xs = [], []
        for q in range(group):
            i = g * group + q
            at = pl.ds(pl.multiple_of((i % per_slab) * BLOCK, BLOCK), BLOCK)
            col = pl.ds(pl.multiple_of(i * BLOCK, BLOCK), BLOCK)
            block = full[i // per_slab, at, col]
            lows.append(block)
            xs.append(jnp.where(r_i == c_i, 1.0 / jnp.where(r_i == c_i, block, 1.0), 0.0))
        s = 1
        while s < BLOCK:
            pick = (r_i // (2 * s) == c_i // (2 * s)) & ((r_i // s) % 2 == 1) & ((c_i // s) % 2 == 0)
            mids = [dot(jnp.where(pick, lows[q], 0.0), xs[q]) for q in range(group)]
            xs = [xs[q] - dot(xs[q], mids[q]) for q in range(group)]
            s *= 2
        for q in range(group):
            inv[g * group + q] = xs[q]
        return 0

    lax.fori_loop(0, blocks // group, invert, 0)

    width = min(512, order)

    def wipe(i, _):
        sol_mat[pl.ds(pl.multiple_of(i * 8, 8), 8), :] = jnp.zeros((8, order), f32)
        return 0

    lax.fori_loop(0, order // 8, wipe, 0)
    w_rows = lax.broadcasted_iota(jnp.int32, (BLOCK, width), 0)

    def substitute(i, _):
        at = pl.ds(pl.multiple_of((i % per_slab) * BLOCK, BLOCK), BLOCK)

        def over(j, _):
            col = pl.ds(pl.multiple_of(j * width, width), width)
            right = jnp.where(w_rows + i * BLOCK == slot_column[:, col], 1.0, 0.0)
            right = right - dot(full[i // per_slab, at, :], sol_mat[:, col])
            sol_mat[pl.ds(pl.multiple_of(i * BLOCK, BLOCK), BLOCK), col] = dot(inv[i], right)
            return 0

        lax.fori_loop(0, order // width, over, 0)
        return 0

    lax.fori_loop(0, blocks, substitute, 0)

    take_halo(*halo_z)
    take_halo(*halo_m)
    y_ok = (rows < cy) | ((rows < cy + 4) & (gy < ny - 1)) | ((rows >= cy + 4) & (gy > 0))

    def settle(x, _):
        x_ok = ((x >= LEAD) | (gx > 0)) & ((x < LEAD + cx) | (gx < nx - 1))
        keep = jnp.where(x_ok, 1.0, 0.0)
        cext[x] = jnp.where(y_ok, 0.6 / (mext[0, x] + 2.75), 0.0) * keep
        for c in range(3):
            rext[c, x] = zext[c, x]
            idir[c, x] = jnp.zeros((ey, 128), f32)
        return 0

    lax.fori_loop(0, ex, settle, 0)
    lines, _, _ = collect(0)
    for t in range(n // 8):
        gres[t] = lines[t]
        gdir[t] = jnp.zeros((1, 128), f32)

    strip = 64

    def coarse():
        own = pl.ds(pl.multiple_of((me // 8) * 128, 128), 128)

        def some(i, acc):
            at = pl.ds(pl.multiple_of(i * strip, strip), strip)
            y = jnp.zeros((strip, 128), f32)
            for t in range(order // 128):
                y = y + sol_mat[at, t * 128 : (t + 1) * 128] * gres[t]
            y = jnp.sum(y, axis=1, keepdims=True)
            return acc + jnp.sum(y * sol_mat[at, own], axis=0, keepdims=True)

        line = lax.fori_loop(0, order // strip, some, jnp.zeros((1, 128), f32), unroll=2)
        weights = [
            jnp.sum(jnp.where(lane1 == base + k, line, 0.0), axis=1, keepdims=True)
            for k in range(vectors)
        ]
        spread = [jnp.broadcast_to(w, (8, 128)) for w in weights]

        def correct(x, _):
            for c in range(3):
                for t in range(0, cy, 8):
                    acc = spread[0] * defl[0, c, x, t : t + 8]
                    for k in range(1, vectors):
                        acc = acc + spread[k] * defl[k, c, x, t : t + 8]
                    cor[c, LEAD + x, t : t + 8] = acc
            return 0

        lax.fori_loop(0, cx, correct, 0)

    def iterate(it, carry):
        gamma_prior, step_prior = carry
        slot = lax.rem(it + 1, 2)
        coarse()
        send_halo(*halo_c)

        def start(x, _):
            for c in range(3):
                ua[c, x] = cext[x] * rext[c, x]
            return 0

        lax.fori_loop(LEAD - 3, LEAD + cx + 3, start, 0)

        def sweep(src, dst):
            def use(x, off, carry):
                for c in range(3):
                    dst[c, x] = 0.4 * src[c, x] + cext[x] * (rext[c, x] + off[c])
                return carry
            return use

        exchange_columns(ua, 0, LEAD - 3, LEAD + cx + 3)
        off_diagonal(ua, 0, LEAD - 2, LEAD + cx + 2, sweep(ua, ub), 0)
        exchange_columns(ub, 1, LEAD - 2, LEAD + cx + 2)
        off_diagonal(ub, 1, LEAD - 1, LEAD + cx + 1, sweep(ub, uz), 0)
        take_halo(*halo_c)

        def join(x, _):
            for c in range(3):
                uz[c, x] = uz[c, x] + cor[c, x]
            return 0

        lax.fori_loop(LEAD - 1, LEAD + cx + 1, join, 0)
        exchange_columns(uz, 2, LEAD - 1, LEAD + cx + 1)

        def image(x, off, carry):
            gam, ene = carry
            diag = mext[0, x, 0:cy] + 2.75
            for c in range(3):
                z = uz[c, x, 0:cy]
                a = diag * z - off[c][0:cy]
                zext[c, x, 0:cy] = a
                gam = gam + rext[c, x, 0:cy] * z
                ene = ene + z * a
            return gam, ene

        nothing = jnp.zeros((cy, 128), f32)
        gam, ene = off_diagonal(uz, 2, LEAD, LEAD + cx, image, (nothing, nothing))
        gam = jnp.sum(jnp.sum(gam, axis=0, keepdims=True), axis=1, keepdims=True)
        ene = jnp.sum(jnp.sum(ene, axis=0, keepdims=True), axis=1, keepdims=True)

        @pl.when(it < ITERS - 1)
        def _():
            send_halo(*halo_z)

        share(slot, gam, ene)
        lines, gamma, energy = collect(slot)
        momentum = jnp.where(it == 0, 0.0, gamma / gamma_prior)
        step = gamma / (energy - momentum * gamma / step_prior)

        @pl.when(it < ITERS - 1)
        def _():
            take_halo(*halo_z)

        def update(x, _):
            for c in range(3):
                image_dir = zext[c, x] + momentum * idir[c, x]
                idir[c, x] = image_dir
                rext[c, x] = rext[c, x] - step * image_dir
            return 0

        lax.fori_loop(LEAD - 3, LEAD + cx + 3, update, 0)

        def advance(x, _):
            for c in range(3):
                d = uz[c, LEAD + x, 0:cy] + momentum * direc[c, x]
                direc[c, x] = d
                sol[c, x] = sol[c, x] + step * d
            return 0

        lax.fori_loop(0, cx, advance, 0)
        for t in range(n // 8):
            image_line = lines[t] + momentum * gdir[t]
            gdir[t] = image_line
            gres[t] = gres[t] - step * image_line
        return gamma, step

    one = jnp.ones((1, 1), f32)
    lax.fori_loop(0, ITERS, iterate, (one, one))

    def give(x, _):
        for c in range(3):
            res[c, x] = rext[c, LEAD + x, 0:cy]
        return 0

    lax.fori_loop(0, cx, give, 0)


def solution(mesh):
    nx, ny, nz = mesh.shape["gx"], mesh.shape["gy"], mesh.shape["gz"]

    def body(forces, mass_shift, deflation, coarse_factor, coarse_slot):
        vectors = deflation.shape[0]
        cx, cy = forces.shape[1], forces.shape[2]
        order = coarse_factor.shape[1]
        slab = coarse_factor.shape[0]
        n = nx * ny * nz
        slot_column = (
            coarse_slot[:, None] * vectors + jnp.arange(vectors, dtype=jnp.int32)[None, :]
        ).reshape(1, -1)
        ex, ey = cx + 2 * LEAD, cy + 8
        f32 = jnp.float32
        vm = lambda *shape: pltpu.VMEM(shape, f32)
        packs = lambda c: [
            vm(c, cx // 2, 8, 128), vm(c, cx // 2, 8, 128),
            vm(c, ex // 2, 8, 128), vm(c, ex // 2, 8, 128),
        ]
        field = (3, ex, ey, 128)
        dma = pltpu.SemaphoreType.DMA
        return pl.pallas_call(
            functools.partial(kernel, (nx, ny, nz, cx, cy, vectors, order)),
            out_shape=[jax.ShapeDtypeStruct(forces.shape, f32)] * 3,
            in_specs=[pl.BlockSpec(memory_space=pltpu.VMEM)] * 5,
            out_specs=[pl.BlockSpec(memory_space=pltpu.VMEM)] * 3,
            scratch_shapes=[
                vm(*field), vm(*field), vm(*field), vm(ex, ey, 128), vm(1, ex, ey, 128),
                vm(*field), vm(*field), vm(*field), vm(*field), vm(ex, ey, 128),
                *packs(3), *packs(3), *packs(1),
                vm(3, 2, 3, ey, 128), vm(3, 2, 3, ey, 128), vm(2, ey, 128),
                vm(nz, slab, order), vm(order // BLOCK, BLOCK, BLOCK), vm(order, order),
                vm(2, 2, 128), vm(2, n, 2, 128), vm(n // 8, 1, 128), vm(n // 8, 1, 128),
                dma((8,)), dma((8,)), dma((8,)), dma((8,)), dma((8,)), dma((8,)),
                dma((3, 2)), dma((3, 2)), dma((2,)), dma((2, n)),
                dma((max(nz - 1, 1),)), dma((max(nz - 1, 1),)), dma,
            ],
            compiler_params=pltpu.CompilerParams(
                collective_id=0, has_side_effects=True, vmem_limit_bytes=66 * 1000 * 1000
            ),
        )(forces, mass_shift, deflation, coarse_factor, slot_column)

    return jax.shard_map(
        body,
        mesh=mesh,
        in_specs=(
            P(None, "gx", "gy", "gz"),
            P("gx", "gy", "gz"),
            P(None, None, "gx", "gy", "gz"),
            P("gz", None),
            P(),
        ),
        out_specs=(P(None, "gx", "gy", "gz"), P(None, "gx", "gy", "gz"), P(None, "gx", "gy", "gz")),
        check_vma=False,
    )
```

time: 912 us -> 135 us (0.15); the launches traced: 900 us -> 134 us
  blocking collectives: 369 us -> 0 us
  starting transfers between devices: 216 us -> 0 us
  Pallas kernels: 0 us -> 127 us
  local copies, waits for them, and re-layouts: 102 us -> 5.96 us
  matrix products: 91.4 us -> 0 us
  other arithmetic: 83.8 us -> 0.73 us
  waiting for transfers between devices: 20.2 us -> 0 us
  between operations: 17.1 us -> 0.64 us
    ppermute x76 -> x0, starting transfers between devices: 216 us -> none  [the longest x36 164 us: with_halo(): lax.ppermute(tail, axis, [(i, (i + 1) % count) for i in range(ends)])]
    psum x12 -> x0, blocking collectives: 195 us -> none  [the longest x4 175 us: body(): lax.psum((jnp.sum(residual * preconditioned), jnp.sum(preconditioned * z_...]
    unnamed x4 -> x0, blocking collectives: 167 us -> none
    pallas_call x0 -> x1, Pallas kernels: none -> 127 us  [body(): pl.pallas_call(functools.partial(kernel, (nx, ny, nz, cx, cy, vectors, or...]
    dot_general x21 -> x0, matrix products: 82.4 us -> none  [the longest x4 48.7 us: body(): local_sums = jnp.dot(flat_vectors, residual.reshape(-1), precision=highest)]
    unnamed x174 -> x3, local copies, waits for them, and re-layouts: 46.4 us -> 5.3 us
    ppermute x24 -> x0, local copies, waits for them, and re-layouts: 38.5 us -> none  [the longest x12 19.3 us: with_halo(): lax.ppermute(head, axis, [((i + 1) % count, i) for i in range(ends)])]
    concatenate x48 -> x0, other arithmetic: 37.7 us -> none  [with_halo(): jnp.concatenate([lax.ppermute(tail, axis, [(i, (i + 1) % count) for i in...]
  transfers between devices with their start and end apart: 76 -> 0, of which waited for: 16 -> 0; matrix products, arithmetic and copies ran while one was open for 9% -> 0% of each run, Pallas kernels for 0% -> 0%
where the time goes in v1:
time: 135 us; the launch traced here: 134 us
  Pallas kernels  127 us (94%)
  local copies, waits for them, and re-layouts  5.96 us (4%)
    pallas_call x1, Pallas kernels, body(): pl.pallas_call(functools.partial(kernel, (nx, ny, nz, cx, cy, vectors, or...  127 us
    unnamed x3, local copies, waits for them, and re-layouts  5.3 us

profile of v1, /device:TPU:0, one launch (start us, length us, event | category | flops | bytes accessed | tf_op | source)
XLA Modules:
  0.0 134.4 jit_solution(16577237578633343006)
XLA Ops:
  0.6 0.7 broadcast_multiply_fusion
  1.3 0.1 iota_add_fusion
  1.4 0.7 add.26.slot_column
  2.0 127.1 %shard_map.76 = (f32[3,16,16,128]{3,2,1,0:T(8,128)}, f32[3,16,16,128]{3,2,1,0:T(8,128)}, f32[3,16,16,128]{3,2,1,0:T(8,128)}) custom-call(f32[3,16,16,128]{3,2,1,0:T(8,128)} %forces.1, f32[16,16,128]{2,1,0:T(8,128)} %mass.1, f32[16,3,16,16,128]{4,3,2,1,0:T(8,128)} %defl.1, f32[256,512]{1,0:T(8,128)} %factor.1, s32[1,512]{1,0:T(1,128)} %add.26.slot_column), custom_call_target="tpu_custom_call" | custom-call | tf_op jit(solution)/shard_map/pallas_call | solution.py:529
  129.1 1.8 %copy.11 = f32[3,16,16,128]{3,2,1,0:T(8,128)} copy(f32[3,16,16,128]{3,2,1,0:T(8,128)} %get-tuple-element.6) | data formatting | bytes 786432
  130.9 1.8 %copy.12 = f32[3,16,16,128]{3,2,1,0:T(8,128)} copy(f32[3,16,16,128]{3,2,1,0:T(8,128)} %get-tuple-element.7) | data formatting | bytes 786432
  132.6 1.8 %copy.13 = f32[3,16,16,128]{3,2,1,0:T(8,128)} copy(f32[3,16,16,128]{3,2,1,0:T(8,128)} %get-tuple-element.8) | data formatting | bytes 786432

commit v2 on v1

--- a/solution.py
+++ b/solution.py
@@ -23,16 +23,16 @@
 
 def kernel(
     sizes,
-    forces, mass, defl, factor, slot_column,
+    forces, mass, defl_hbm, factor, slot_column,
     sol, res, direc,
     zext, rext, idir, cext, mext, cor, ua, ub, uz, vx,
     low, high, got_low, got_high,
     low_c, high_c, got_low_c, got_high_c,
     low_m, high_m, got_low_m, got_high_m,
-    zsend, zgot, vzb,
+    zsend, zgot, vzb, defl,
     full, inv, sol_mat, gsend, gat, gres, gdir,
     zx_send, zx_recv, c_send, c_recv, m_send, m_recv,
-    zc_send, zc_recv, g_send, g_recv, f_send, f_recv, f_local,
+    zc_send, zc_recv, g_send, g_recv, f_send, f_recv, f_local, d_local,
 ):
     nx, ny, nz, cx, cy, vectors, order = sizes
     n = nx * ny * nz
@@ -50,7 +50,12 @@
     rows = lax.broadcasted_iota(jnp.int32, (ey, 128), 0)
     lane1 = lax.broadcasted_iota(jnp.int32, (1, 128), 1)
 
-    for ref in (zext, cor, mext, got_low, got_high, got_low_c, got_high_c, got_low_m, got_high_m):
+    load = pltpu.make_async_copy(defl_hbm, defl, d_local)
+    load.start()
+    for ref in (
+        zext.at[0], zext.at[1], got_low.at[0], got_low.at[1], got_high.at[0], got_high.at[1],
+        cor, mext, got_low_c, got_high_c, got_low_m, got_high_m,
+    ):
         lead = ref.shape[0]
         for c in range(lead):
             def clear(i, _, ref=ref, c=c):
@@ -152,9 +157,65 @@
 
         lax.fori_loop(0, ex // 2, unpack, 0)
 
-    halo_z = (zext, low, high, got_low, got_high, zx_send, zx_recv)
-    halo_c = (cor, low_c, high_c, got_low_c, got_high_c, c_send, c_recv)
+    def halo_z(slot):
+        return (
+            zext.at[slot], low, high, got_low.at[slot], got_high.at[slot],
+            zx_send, zx_recv.at[slot],
+        )
+
     halo_m = (mext, low_m, high_m, got_low_m, got_high_m, m_send, m_recv)
+
+    eighth = cx // 8
+
+    def thin_pieces():
+        out = []
+        for d, (dx, dy) in enumerate(DIRS):
+            if dy == 0:
+                src = cor.at[:, pl.ds(LEAD if dx < 0 else LEAD + cx - 1, 1), pl.ds(0, cy)]
+                dst = cor.at[:, pl.ds(LEAD + cx if dx < 0 else LEAD - 1, 1), pl.ds(0, cy)]
+            else:
+                start, count = {0: (0, eighth), -1: (0, 1), 1: (eighth - 1, 1)}[dx]
+                to = {0: 1, -1: 1 + eighth, 1: 0}[dx]
+                src = (low_c if dy < 0 else high_c).at[:, pl.ds(start, count)]
+                dst = (got_low_c if dy < 0 else got_high_c).at[:, pl.ds(to, count)]
+            copy = pltpu.make_async_remote_copy(
+                src_ref=src,
+                dst_ref=dst,
+                send_sem=c_send.at[d],
+                recv_sem=c_recv.at[d],
+                device_id={"gx": gx + dx, "gy": gy + dy, "gz": gz},
+                device_id_type=MESH,
+            )
+            out.append((dx, dy, copy))
+        return out
+
+    def send_thin():
+        for c in range(3):
+            for t in range(eighth):
+                lo = hi = jnp.zeros((8, 128), f32)
+                for j in range(8):
+                    x = LEAD + 8 * t + j
+                    lo = jnp.where(row8 == j, pltpu.roll(cor[c, x, 0:8], j, 0) if j else cor[c, x, 0:8], lo)
+                    a = cor[c, x, cy - 8 : cy]
+                    hi = jnp.where(row8 == j, pltpu.roll(a, (j + 1) % 8, 0) if j < 7 else a, hi)
+                low_c[c, t] = lo
+                high_c[c, t] = hi
+        for dx, dy, copy in thin_pieces():
+            pl.when(exists(dx, dy))(copy.start)
+
+    def take_thin():
+        for dx, dy, copy in thin_pieces():
+            pl.when(exists(-dx, -dy))(copy.wait_recv)
+            pl.when(exists(dx, dy))(copy.wait_send)
+        for c in range(3):
+            for t in range(eighth + 2):
+                a, b = got_low_c[c, t], got_high_c[c, t]
+                for j in range(8):
+                    x = LEAD - 8 + 8 * t + j
+                    if LEAD - 1 <= x <= LEAD + cx:
+                        p = pltpu.roll(a, 8 - j, 0) if j else a
+                        q = pltpu.roll(b, 7 - j, 0) if j < 7 else b
+                        cor[c, x, cy : cy + 8] = jnp.where(row8 < 4, p, q)
 
     def columns(stage, side):
         return pltpu.make_async_remote_copy(
@@ -168,7 +229,7 @@
 
     has = (gz > 0, gz < nz - 1)
 
-    def exchange_columns(u, stage, first, last):
+    def send_columns(u, stage, first, last):
         for side in (0, 1):
             @pl.when(has[side])
             def _(side=side):
@@ -182,6 +243,8 @@
                 for c in range(3):
                     zsend[stage, side, c] = acc[c]
                 columns(stage, side).start()
+
+    def take_columns(stage):
         for side in (0, 1):
             pl.when(has[1 - side])(columns(stage, side).wait_recv)
             pl.when(has[side])(columns(stage, side).wait_send)
@@ -191,6 +254,10 @@
                 pltpu.roll(bx, 127, 1) - pltpu.roll(bx, 1, 1)
                 + pltpu.roll(by, ey - 1, 0) - pltpu.roll(by, 1, 0)
             )
+
+    def exchange_columns(u, stage, first, last):
+        send_columns(u, stage, first, last)
+        take_columns(stage)
 
     def y_pair(v):
         return pltpu.roll(v, ey - 1, 0), pltpu.roll(v, 1, 0)
@@ -237,7 +304,7 @@
         def part(x, acc):
             acc = list(acc)
             for c in range(3):
-                v = zext[c, LEAD + x, 0:cy]
+                v = zext[slot, c, LEAD + x, 0:cy]
                 for k in range(vectors):
                     prod = defl[k, c, x] * v
                     for t in range(0, cy, 8):
@@ -290,15 +357,16 @@
 
     def fill(x, _):
         for c in range(3):
-            zext[c, LEAD + x, 0:cy] = forces[c, x]
+            zext[0, c, LEAD + x, 0:cy] = forces[c, x]
             sol[c, x] = jnp.zeros((cy, 128), f32)
             direc[c, x] = jnp.zeros((cy, 128), f32)
         mext[0, LEAD + x, 0:cy] = mass[x]
         return 0
 
     lax.fori_loop(0, cx, fill, 0)
-    send_halo(*halo_z)
+    send_halo(*halo_z(0))
     send_halo(*halo_m)
+    load.wait()
     zero = jnp.zeros((1, 1), f32)
     share(0, zero, zero)
 
@@ -358,20 +426,6 @@
 
     lax.fori_loop(0, blocks, substitute, 0)
 
-    take_halo(*halo_z)
-    take_halo(*halo_m)
-    y_ok = (rows < cy) | ((rows < cy + 4) & (gy < ny - 1)) | ((rows >= cy + 4) & (gy > 0))
-
-    def settle(x, _):
-        x_ok = ((x >= LEAD) | (gx > 0)) & ((x < LEAD + cx) | (gx < nx - 1))
-        keep = jnp.where(x_ok, 1.0, 0.0)
-        cext[x] = jnp.where(y_ok, 0.6 / (mext[0, x] + 2.75), 0.0) * keep
-        for c in range(3):
-            rext[c, x] = zext[c, x]
-            idir[c, x] = jnp.zeros((ey, 128), f32)
-        return 0
-
-    lax.fori_loop(0, ex, settle, 0)
     lines, _, _ = collect(0)
     for t in range(n // 8):
         gres[t] = lines[t]
@@ -408,12 +462,26 @@
 
         lax.fori_loop(0, cx, correct, 0)
 
+    coarse()
+    send_thin()
+    take_halo(*halo_z(0))
+    take_halo(*halo_m)
+    y_ok = (rows < cy) | ((rows < cy + 4) & (gy < ny - 1)) | ((rows >= cy + 4) & (gy > 0))
+
+    def settle(x, _):
+        x_ok = ((x >= LEAD) | (gx > 0)) & ((x < LEAD + cx) | (gx < nx - 1))
+        keep = jnp.where(x_ok, 1.0, 0.0)
+        cext[x] = jnp.where(y_ok, 0.6 / (mext[0, x] + 2.75), 0.0) * keep
+        for c in range(3):
+            rext[c, x] = zext[0, c, x]
+            idir[c, x] = jnp.zeros((ey, 128), f32)
+        return 0
+
+    lax.fori_loop(0, ex, settle, 0)
+
     def iterate(it, carry):
         gamma_prior, step_prior = carry
         slot = lax.rem(it + 1, 2)
-        coarse()
-        send_halo(*halo_c)
-
         def start(x, _):
             for c in range(3):
                 ua[c, x] = cext[x] * rext[c, x]
@@ -432,7 +500,7 @@
         off_diagonal(ua, 0, LEAD - 2, LEAD + cx + 2, sweep(ua, ub), 0)
         exchange_columns(ub, 1, LEAD - 2, LEAD + cx + 2)
         off_diagonal(ub, 1, LEAD - 1, LEAD + cx + 1, sweep(ub, uz), 0)
-        take_halo(*halo_c)
+        take_thin()
 
         def join(x, _):
             for c in range(3):
@@ -448,7 +516,7 @@
             for c in range(3):
                 z = uz[c, x, 0:cy]
                 a = diag * z - off[c][0:cy]
-                zext[c, x, 0:cy] = a
+                zext[slot, c, x, 0:cy] = a
                 gam = gam + rext[c, x, 0:cy] * z
                 ene = ene + z * a
             return gam, ene
@@ -460,38 +528,44 @@
 
         @pl.when(it < ITERS - 1)
         def _():
-            send_halo(*halo_z)
+            send_halo(*halo_z(slot))
 
         share(slot, gam, ene)
         lines, gamma, energy = collect(slot)
         momentum = jnp.where(it == 0, 0.0, gamma / gamma_prior)
         step = gamma / (energy - momentum * gamma / step_prior)
 
-        @pl.when(it < ITERS - 1)
-        def _():
-            take_halo(*halo_z)
-
-        def update(x, _):
-            for c in range(3):
-                image_dir = zext[c, x] + momentum * idir[c, x]
-                idir[c, x] = image_dir
-                rext[c, x] = rext[c, x] - step * image_dir
-            return 0
-
-        lax.fori_loop(LEAD - 3, LEAD + cx + 3, update, 0)
-
-        def advance(x, _):
-            for c in range(3):
-                d = uz[c, LEAD + x, 0:cy] + momentum * direc[c, x]
-                direc[c, x] = d
-                sol[c, x] = sol[c, x] + step * d
-            return 0
-
-        lax.fori_loop(0, cx, advance, 0)
         for t in range(n // 8):
             image_line = lines[t] + momentum * gdir[t]
             gdir[t] = image_line
             gres[t] = gres[t] - step * image_line
+
+        @pl.when(it < ITERS - 1)
+        def _():
+            coarse()
+            send_thin()
+
+        def advance(x, _):
+            for c in range(3):
+                d = uz[c, LEAD + x, 0:cy] + momentum * direc[c, x]
+                direc[c, x] = d
+                sol[c, x] = sol[c, x] + step * d
+            return 0
+
+        lax.fori_loop(0, cx, advance, 0)
+
+        @pl.when(it < ITERS - 1)
+        def _():
+            take_halo(*halo_z(slot))
+
+        def update(x, _):
+            for c in range(3):
+                image_dir = zext[slot, c, x] + momentum * idir[c, x]
+                idir[c, x] = image_dir
+                rext[c, x] = rext[c, x] - step * image_dir
+            return 0
+
+        lax.fori_loop(LEAD - 3, LEAD + cx + 3, update, 0)
         return gamma, step
 
     one = jnp.ones((1, 1), f32)
@@ -529,18 +603,24 @@
         return pl.pallas_call(
             functools.partial(kernel, (nx, ny, nz, cx, cy, vectors, order)),
             out_shape=[jax.ShapeDtypeStruct(forces.shape, f32)] * 3,
-            in_specs=[pl.BlockSpec(memory_space=pltpu.VMEM)] * 5,
+            in_specs=[
+                pl.BlockSpec(memory_space=pl.ANY if i == 2 else pltpu.VMEM) for i in range(5)
+            ],
             out_specs=[pl.BlockSpec(memory_space=pltpu.VMEM)] * 3,
             scratch_shapes=[
-                vm(*field), vm(*field), vm(*field), vm(ex, ey, 128), vm(1, ex, ey, 128),
+                vm(2, *field), vm(*field), vm(*field), vm(ex, ey, 128), vm(1, ex, ey, 128),
                 vm(*field), vm(*field), vm(*field), vm(*field), vm(ex, ey, 128),
-                *packs(3), *packs(3), *packs(1),
-                vm(3, 2, 3, ey, 128), vm(3, 2, 3, ey, 128), vm(2, ey, 128),
+                vm(3, cx // 2, 8, 128), vm(3, cx // 2, 8, 128),
+                vm(2, 3, ex // 2, 8, 128), vm(2, 3, ex // 2, 8, 128),
+                vm(3, cx // 8, 8, 128), vm(3, cx // 8, 8, 128),
+                vm(3, cx // 8 + 2, 8, 128), vm(3, cx // 8 + 2, 8, 128),
+                *packs(1),
+                vm(3, 2, 3, ey, 128), vm(3, 2, 3, ey, 128), vm(2, ey, 128), vm(*deflation.shape),
                 vm(nz, slab, order), vm(order // BLOCK, BLOCK, BLOCK), vm(order, order),
                 vm(2, 2, 128), vm(2, n, 2, 128), vm(n // 8, 1, 128), vm(n // 8, 1, 128),
-                dma((8,)), dma((8,)), dma((8,)), dma((8,)), dma((8,)), dma((8,)),
+                dma((8,)), dma((2, 8)), dma((8,)), dma((8,)), dma((8,)), dma((8,)),
                 dma((3, 2)), dma((3, 2)), dma((2,)), dma((2, n)),
-                dma((max(nz - 1, 1),)), dma((max(nz - 1, 1),)), dma,
+                dma((max(nz - 1, 1),)), dma((max(nz - 1, 1),)), dma, dma,
             ],
             compiler_params=pltpu.CompilerParams(
                 collective_id=0, has_side_effects=True, vmem_limit_bytes=66 * 1000 * 1000

time: 135 us -> 133 us (0.985)
    pallas_call x1, Pallas kernels: 127 us -> 126 us  [body(): pl.pallas_call(functools.partial(kernel, (nx, ny, nz, cx, cy, vectors, or...]
where the time goes in v2:
time: 133 us
  Pallas kernels  126 us (95%)
  local copies, waits for them, and re-layouts  5.96 us (4%)
    pallas_call x1, Pallas kernels, body(): pl.pallas_call(functools.partial(kernel, (nx, ny, nz, cx, cy, vectors, or...  126 us
    unnamed x3, local copies, waits for them, and re-layouts  5.3 us

profile of v2, /device:TPU:0, one launch (start us, length us, event | category | flops | bytes accessed | tf_op | source)
XLA Modules:
  0.0 132.8 jit_solution(10986009970259132117)
XLA Ops:
  0.6 0.7 broadcast_multiply_fusion
  1.3 0.1 iota_add_fusion
  1.4 0.7 add.26.slot_column
  2.0 125.5 %shard_map.76 = (f32[3,16,16,128]{3,2,1,0:T(8,128)}, f32[3,16,16,128]{3,2,1,0:T(8,128)}, f32[3,16,16,128]{3,2,1,0:T(8,128)}) custom-call(f32[3,16,16,128]{3,2,1,0:T(8,128)} %forces.1, f32[16,16,128]{2,1,0:T(8,128)} %mass.1, f32[16,3,16,16,128]{4,3,2,1,0:T(8,128)} %defl_hbm.1, f32[256,512]{1,0:T(8,128)} %factor.1, s32[1,512]{1,0:T(1,128)} %add.26.slot_column), custom_call_target="tpu_custom_call" | custom-call | tf_op jit(solution)/shard_map/pallas_call | solution.py:603
  127.5 1.8 %copy.11 = f32[3,16,16,128]{3,2,1,0:T(8,128)} copy(f32[3,16,16,128]{3,2,1,0:T(8,128)} %get-tuple-element.6) | data formatting | bytes 786432
  129.3 1.8 %copy.12 = f32[3,16,16,128]{3,2,1,0:T(8,128)} copy(f32[3,16,16,128]{3,2,1,0:T(8,128)} %get-tuple-element.7) | data formatting | bytes 786432
  131.1 1.8 %copy.13 = f32[3,16,16,128]{3,2,1,0:T(8,128)} copy(f32[3,16,16,128]{3,2,1,0:T(8,128)} %get-tuple-element.8) | data formatting | bytes 786432
